TPU v7x, 32 devices: a whole 2x2x4 slice. The times are simulated.
32 devices in a mesh: gx: 2 (over x), gy: 4 (over z), gz: 4 (over y, core).
Axes of the slice: x: 2, y: 2, z: 4, core: 2. Of those that a mesh axis runs over, the one named last changes fastest.
Arguments:
- fields: float32 [4, 8, 256, 512], P(None, 'gx', 'gy', 'gz'), may hold values from -8 to 8
- volume_code: int32 [8, 256, 512], P('gx', 'gy', 'gz'), may hold values from 65536 to 1048576
- cut_flag: int32 [8, 256, 512], P('gx', 'gy', 'gz'), may hold values 0 or 1
- member_bits: int32 [8, 256, 512], P('gx', 'gy', 'gz'), may hold values from 0 to 134217727
Outputs:
- merged: float32 [4, 8, 256, 512], P(None, 'gx', 'gy', 'gz')
All inputs are finite; a program needn't handle non-finite values. No bound on the sum of `cut_flag` on one device may be relied on, other than what follows from the above.
Results may differ from a plain program's by a relative error of at most 0.00015.
Values sent between devices are 32-bit elements; how exact they have to be, the bound alone decides.
A program may use at most 128 MiB of HBM per device.

v0:
```python
import functools

import jax
import jax.numpy as jnp
from jax import lax
from jax.experimental import pallas as pl
from jax.experimental.pallas import tpu as pltpu
from jax.sharding import PartitionSpec as P

PASSES = 2
MESH = pl.DeviceIdType.MESH
AXES = ("gx", "gy", "gz")
SIDES = [(dx, dy) for dx in (-1, 0, 1) for dy in (-1, 0, 1) if (dx, dy) != (0, 0)]
ROWS = 8
SLOT = 8


def bit_of(active, dx, dy, dz):
    index = 9 * (dx + 1) + 3 * (dy + 1) + (dz + 1)
    return jnp.bitwise_and(active, 1 << index) != 0


def ones_in(active):
    v = active - jnp.bitwise_and(jnp.right_shift(active, 1), 0x55555555)
    v = jnp.bitwise_and(v, 0x33333333) + jnp.bitwise_and(jnp.right_shift(v, 2), 0x33333333)
    v = jnp.bitwise_and(v + jnp.right_shift(v, 4), 0x0F0F0F0F)
    v = v + jnp.right_shift(v, 8)
    v = v + jnp.right_shift(v, 16)
    return jnp.bitwise_and(v, 63)


def kernel(
    counts, fields, code, flag, bits, out,
    pull0, push0, pull1, push1, act, volume, inverse, acc, total, shifted, packed, landed,
    side_send, side_recv, act_send, act_recv, z_send, z_recv,
):
    nf, nx, ny, nz = fields.shape
    place = [lax.axis_index(name) for name in AXES]

    def device(dx, dy, dz):
        step = (dx, dy, dz)
        return tuple(
            lax.rem(place[d] + step[d] + counts[d], counts[d]) if step[d] else place[d]
            for d in range(3)
        )

    barrier = pltpu.get_barrier_semaphore()
    for dx, dy in SIDES:
        pl.semaphore_signal(barrier, inc=1, device_id=device(dx, dy, 0), device_id_type=MESH)
    for dz in (-1, 1):
        pl.semaphore_signal(barrier, inc=1, device_id=device(0, 0, dz), device_id_type=MESH)

    lane = lax.broadcasted_iota(jnp.int32, (ROWS, nz), 1)
    chunks = ny // ROWS

    def loop_planes(count, work):
        def step(x, carry):
            work(x)
            return carry
        lax.fori_loop(0, count, step, 0)

    def window(side, size, first):
        if side == 0:
            return pl.ds(first, size), pl.ds(first, size)
        if side > 0:
            return pl.ds(first + size - 1, 1), pl.ds(first - 1, 1)
        return pl.ds(first, 1), pl.ds(first + size, 1)

    def side_copies(ref, lead, send, recv):
        copies = []
        for k, (dx, dy) in enumerate(SIDES):
            from_x, to_x = window(dx, nx, 1)
            from_y, to_y = window(dy, ny, ROWS)
            copies.append(
                pltpu.make_async_remote_copy(
                    src_ref=ref.at[lead + (from_x, from_y)],
                    dst_ref=ref.at[lead + (to_x, to_y)],
                    send_sem=send(k),
                    recv_sem=recv(k),
                    device_id=device(dx, dy, 0),
                    device_id_type=MESH,
                )
            )
        return copies

    def z_copies(turn, group, rows):
        copies = []
        for k, dz in enumerate((1, -1)):
            copies.append(
                pltpu.make_async_remote_copy(
                    src_ref=packed.at[turn, group, k, pl.ds(0, rows)],
                    dst_ref=landed.at[turn, group, k, pl.ds(0, rows)],
                    send_sem=z_send.at[turn, group, k],
                    recv_sem=z_recv.at[turn, group, k],
                    device_id=device(0, 0, dz),
                    device_id_type=MESH,
                )
            )
        return copies

    started = []

    def start(copies):
        for copy in copies:
            copy.start()
        started.extend(copies)

    def arrive(copies):
        for copy in copies:
            copy.wait_recv()

    def turn_copies(turn):
        ref = (pull0, push0, pull1, push1)[turn]
        copies = side_copies(
            ref, (slice(None),), lambda k: side_send.at[turn, k], lambda k: side_recv.at[turn, k]
        )
        sides = SIDES
        if turn == 0:
            copies += side_copies(act, (), lambda k: act_send.at[k], lambda k: act_recv.at[k])
            sides = SIDES + SIDES
        across = [copy for copy, side in zip(copies, sides) if side[0] != 0]
        along = [copy for copy, side in zip(copies, sides) if side[0] == 0]
        return across, along

    ends = sorted({0, nx - 1})

    def inner_planes(work):
        if nx > 2:
            def step(x, carry):
                work(x)
                return carry
            lax.fori_loop(1, nx - 1, step, 0)

    def own(x, sign):
        inside = [dx for dx in (-1, 0, 1) if 0 <= x - sign * dx < nx]
        return inside, [dx for dx in (-1, 0, 1) if dx not in inside]

    def rolled(value, amount):
        return pltpu.roll(value, amount % nz, 1)

    def prepare(x):
        for j in range(chunks):
            rows, inner = pl.ds(ROWS * j, ROWS), pl.ds(ROWS * (j + 1), ROWS)
            kappa = code[x, rows].astype(jnp.float32) * (1.0 / 1048576.0)
            active = bits[x, rows] * flag[x, rows]
            act[x + 1, inner] = active
            pull0[0, x + 1, inner] = kappa
            for c in range(nf):
                pull0[c + 1, x + 1, inner] = kappa * fields[c, x, rows]
            others = ones_in(jnp.bitwise_and(active, ((1 << 27) - 1) ^ (1 << 13)))
            inverse[x, rows] = 1.0 / (1 + others).astype(jnp.float32)

    loop_planes(nx, prepare)
    packed[...] = jnp.zeros_like(packed)
    pl.semaphore_wait(barrier, len(SIDES) + 2)
    flights = [turn_copies(turn) for turn in range(2 * PASSES)]
    start(flights[0][1])
    start(flights[0][0])

    def pull(step):
        ref = (pull0, pull1)[step]
        target = (push0, push1)[step]
        arrays = range(nf + 1) if step == 0 else range(1, nf + 1)
        turn = 2 * step
        base = 0 if step == 0 else 1
        across, along = flights[turn]

        def sums(x, j, dxs, dzs, found):
            for dx in dxs:
                for dy in (-1, 0, 1):
                    rows = pl.ds(ROWS * (j + 1) - dy, ROWS)
                    active = act[x + 1 - dx, rows]
                    values = [ref[c - base, x + 1 - dx, rows] for c in arrays]
                    for dz in dzs:
                        if (dx, dy, dz) == (0, 0, 0):
                            terms = values
                        else:
                            member = bit_of(active, dx, dy, dz)
                            terms = [jnp.where(member, v, 0.0) for v in values]
                        if dz in found:
                            found[dz] = [a + b for a, b in zip(found[dz], terms)]
                        else:
                            found[dz] = terms
            return found

        def pack(x, j, found):
            rows = pl.ds(ROWS * j, ROWS)
            for k, dz in enumerate((1, -1)):
                tile = packed[turn, 0, k, rows]
                for c, value in zip(arrays, found[dz]):
                    acc[k, c, x, rows] = value
                    at = x * SLOT + c
                    tile = jnp.where(lane == at, rolled(value, at + (dz == 1)), tile)
                packed[turn, 0, k, rows] = tile

        def early(x, dxs, complete):
            for j in range(chunks):
                rows = pl.ds(ROWS * j, ROWS)
                found = sums(x, j, dxs, (1, 0, -1), {})
                for c, value in zip(arrays, found[0]):
                    total[c, x, rows] = value
                if complete:
                    pack(x, j, found)
                else:
                    for k, dz in enumerate((1, -1)):
                        for c, value in zip(arrays, found[dz]):
                            acc[k, c, x, rows] = value

        arrive(along)
        inner_planes(lambda x: early(x, (-1, 0, 1), True))
        for x in ends:
            early(x, own(x, 1)[0], False)
        arrive(across)
        for x in ends:
            for j in range(chunks):
                rows = pl.ds(ROWS * j, ROWS)
                found = {dz: [acc[k, c, x, rows] for c in arrays] for k, dz in enumerate((1, -1))}
                pack(x, j, sums(x, j, own(x, 1)[1], (1, -1), found))
        copies = z_copies(turn, 0, ny)
        start(copies)
        for x in ends:
            for j in range(chunks):
                rows = pl.ds(ROWS * j, ROWS)
                found = {0: [total[c, x, rows] for c in arrays]}
                for c, value in zip(arrays, sums(x, j, own(x, 1)[1], (0,), found)[0]):
                    total[c, x, rows] = value
        arrive(copies)

        def finish(x):
            for j in range(chunks):
                rows, inner = pl.ds(ROWS * j, ROWS), pl.ds(ROWS * (j + 1), ROWS)
                low, high = landed[turn, 0, 0, rows], landed[turn, 0, 1, rows]
                found = {}
                for c in arrays:
                    at = x * SLOT + c
                    from_low = jnp.where(lane == 0, rolled(low, nz - at), rolled(acc[0, c, x, rows], 1))
                    from_high = jnp.where(
                        lane == nz - 1, rolled(high, nz - 1 - at), rolled(acc[1, c, x, rows], nz - 1)
                    )
                    found[c] = total[c, x, rows] + from_low + from_high
                if step == 0:
                    scale = 1.0 / found[0]
                    volume[x, rows] = scale
                else:
                    scale = volume[x, rows]
                for c in range(nf):
                    target[c, x + 1, inner] = found[c + 1] * scale

        for x in ends:
            finish(x)
        start(flights[turn + 1][0])
        inner_planes(finish)
        start(flights[turn + 1][1])

    def push(step):
        ref = (push0, push1)[step]
        turn = 2 * step + 1
        across, along = flights[turn]

        def columns(group, x):
            for j in range(chunks + 2):
                rows = pl.ds(ROWS * j, ROWS)
                for k, dz in enumerate((1, -1)):
                    tile = packed[turn, group, k, rows]
                    for c in range(nf):
                        at = x * SLOT + c
                        tile = jnp.where(lane == at, rolled(ref[c, x, rows], at + (dz == 1)), tile)
                    packed[turn, group, k, rows] = tile

        def shift(group, x):
            for j in range(chunks + 2):
                rows = pl.ds(ROWS * j, ROWS)
                low, high = landed[turn, group, 0, rows], landed[turn, group, 1, rows]
                for c in range(nf):
                    at = x * SLOT + c
                    value = ref[c, x, rows]
                    shifted[0, c, x, rows] = jnp.where(lane == 0, rolled(low, nz - at), rolled(value, 1))
                    shifted[1, c, x, rows] = jnp.where(
                        lane == nz - 1, rolled(high, nz - 1 - at), rolled(value, nz - 1)
                    )

        def planes(first, count, work):
            def step(x, carry):
                work(x)
                return carry
            lax.fori_loop(first, first + count, step, 0)

        def gathered(x, j, dxs, dzs, values):
            active = act[x + 1, pl.ds(ROWS * (j + 1), ROWS)]
            for dz in dzs:
                for dx in dxs:
                    for dy in (-1, 0, 1):
                        rows = pl.ds(ROWS * (j + 1) + dy, ROWS)
                        if dz == 0:
                            terms = [ref[c, x + 1 + dx, rows] for c in range(nf)]
                        else:
                            terms = [shifted[(dz + 1) // 2, c, x + 1 + dx, rows] for c in range(nf)]
                        if (dx, dy, dz) != (0, 0, 0):
                            member = bit_of(active, dx, dy, dz)
                            terms = [jnp.where(member, v, 0.0) for v in terms]
                        values = terms if values is None else [a + b for a, b in zip(values, terms)]
            return values

        def held(x, j):
            return [total[c, x, pl.ds(ROWS * j, ROWS)] for c in range(nf)]

        def keep(x, j, values):
            for c in range(nf):
                total[c, x, pl.ds(ROWS * j, ROWS)] = values[c]

        def give(x, j, values):
            rows, inner = pl.ds(ROWS * j, ROWS), pl.ds(ROWS * (j + 1), ROWS)
            scale = inverse[x, rows]
            if step == PASSES - 1:
                for c in range(nf):
                    out[c, x, rows] = values[c] * scale
            else:
                scale = scale * pull0[0, x + 1, inner]
                for c in range(nf):
                    pull1[c, x + 1, inner] = values[c] * scale

        def add(x, dxs, dzs, first, last):
            for j in range(chunks):
                values = gathered(x, j, dxs, dzs, None if first else held(x, j))
                (give if last else keep)(x, j, values)

        arrive(along)
        planes(1, nx, lambda x: columns(0, x))
        copies = z_copies(turn, 0, ny + 2 * ROWS)
        start(copies)
        inner_planes(lambda x: add(x, (-1, 0, 1), (0,), True, False))
        for x in ends:
            add(x, own(x, -1)[0], (0,), True, False)
        arrive(copies)
        planes(1, nx, lambda x: shift(0, x))
        for x in ends:
            add(x, own(x, -1)[0], (-1, 1), False, False)
        inner_planes(lambda x: add(x, (-1, 0, 1), (-1, 1), False, True))
        arrive(across)
        for x in (0, nx + 1):
            columns(1, x)
        copies = z_copies(turn, 1, ny + 2 * ROWS)
        start(copies)
        for x in ends:
            add(x, own(x, -1)[1], (0,), False, False)
        arrive(copies)
        for x in (0, nx + 1):
            shift(1, x)
        for x in ends:
            add(x, own(x, -1)[1], (-1, 1), False, True)
        if step < PASSES - 1:
            start(flights[turn + 1][1])
            start(flights[turn + 1][0])

    for step in range(PASSES):
        pull(step)
        push(step)
    for copy in started:
        copy.wait_send()


def body(counts, fields, code, flag, bits):
    nf, nx, ny, nz = fields.shape
    frame = (nx + 2, ny + 2 * ROWS, nz)
    turns = 2 * PASSES
    vmem = pl.BlockSpec(memory_space=pltpu.VMEM)
    f32 = jnp.float32
    return pl.pallas_call(
        functools.partial(kernel, counts),
        out_shape=jax.ShapeDtypeStruct(fields.shape, f32),
        in_specs=[vmem] * 4,
        out_specs=vmem,
        scratch_shapes=[
            pltpu.VMEM((nf + 1,) + frame, f32),
            pltpu.VMEM((nf,) + frame, f32),
            pltpu.VMEM((nf,) + frame, f32),
            pltpu.VMEM((nf,) + frame, f32),
            pltpu.VMEM(frame, jnp.int32),
            pltpu.VMEM((nx, ny, nz), f32),
            pltpu.VMEM((nx, ny, nz), f32),
            pltpu.VMEM((2, nf + 1, nx, ny, nz), f32),
            pltpu.VMEM((nf + 1, nx, ny, nz), f32),
            pltpu.VMEM((2, nf) + frame, f32),
            pltpu.VMEM((turns, 2, 2, ny + 2 * ROWS, nz), f32),
            pltpu.VMEM((turns, 2, 2, ny + 2 * ROWS, nz), f32),
            pltpu.SemaphoreType.DMA((turns, len(SIDES))),
            pltpu.SemaphoreType.DMA((turns, len(SIDES))),
            pltpu.SemaphoreType.DMA((len(SIDES),)),
            pltpu.SemaphoreType.DMA((len(SIDES),)),
            pltpu.SemaphoreType.DMA((turns, 2, 2)),
            pltpu.SemaphoreType.DMA((turns, 2, 2)),
        ],
        compiler_params=pltpu.CompilerParams(collective_id=0, has_side_effects=True),
    )(fields, code, flag, bits)


def solution(mesh):
    counts = tuple(mesh.shape[name] for name in AXES)
    spec = P("gx", "gy", "gz")
    whole = P(None, "gx", "gy", "gz")
    return jax.shard_map(
        functools.partial(body, counts),
        mesh=mesh,
        in_specs=(whole, spec, spec, spec),
        out_specs=whole,
        check_vma=False,
    )
```

profile of v0, /device:TPU:0, one launch (start us, length us, event | category | flops | bytes accessed | tf_op | source)
XLA Modules:
  0.0 59.1 jit_solution(15160597334326769220)
XLA Ops:
  0.0 57.2 %shard_map.46 = f32[4,4,64,128]{3,2,1,0:T(8,128)} custom-call(f32[4,4,64,128]{3,2,1,0:T(8,128)} %fields.1, s32[4,64,128]{2,1,0:T(8,128)} %code.1, s32[4,64,128]{2,1,0:T(8,128)} %flag.1, s32[4,64,128]{2,1,0:T(8,128)} %bits.1), custom_call_target="tpu_custom_call" | custom-call | tf_op jit(solution)/shard_map/pallas_call | solution.py:368
  57.2 1.9 %copy.6 = f32[4,4,64,128]{3,2,1,0:T(8,128)} copy(f32[4,4,64,128]{3,2,1,0:T(8,128)} %shard_map.46) | data formatting | bytes 1048576
where the time goes:
time: 59.3 us; the launch traced here: 59.1 us
  Pallas kernels  57.2 us (96%)
  local copies, waits for them, and re-layouts  1.89 us (3%)
    pallas_call x1, Pallas kernels, body(): pl.pallas_call(functools.partial(kernel, counts), out_shape=jax.ShapeDtyp...  57.2 us
    unnamed x1, local copies, waits for them, and re-layouts  1.89 us

commit v1 on v0

--- a/solution.py
+++ b/solution.py
@@ -13,6 +13,8 @@
 SIDES = [(dx, dy) for dx in (-1, 0, 1) for dy in (-1, 0, 1) if (dx, dy) != (0, 0)]
 ROWS = 8
 SLOT = 8
+REACH = 2 * PASSES
+GROUP = 4 * REACH
 
 
 def bit_of(active, dx, dy, dz):
@@ -394,12 +396,468 @@
     )(fields, code, flag, bits)
 
 
+def folded_kernel(
+    counts, fields, code, flag, bits, out,
+    raw, rawcode, bit_box, flag_box, act_box, act, pull0, push0, pull1, push1,
+    edge_act, edge0, edge1, edge2, edge3, ends, act_ends,
+    volume, inverse, weight, edge_volume, edge_weight,
+    packed, act_packed, landed, act_landed, done,
+    load_sem, x_send, x_recv, y_send, y_recv, z_send, z_recv, back_send, back_recv, own_sem,
+):
+    nf, nx, ny, nz = fields.shape
+    planes = 2 * nx
+    half = ny // 2
+    tiles = (half + 2 * REACH) // ROWS
+    place = [lax.axis_index(name) for name in AXES]
+    side = place[0]
+    last = ny - REACH
+    top, bottom = ROWS, ROWS + REACH + half
+
+    def device(dx, dy, dz):
+        step = (dx, dy, dz)
+        return tuple(
+            lax.rem(place[d] + step[d] + counts[d], counts[d]) if step[d] else place[d]
+            for d in range(3)
+        )
+
+    def by_side(work):
+        for s in (0, 1):
+            @pl.when(side == s)
+            def _(s=s):
+                work(s)
+
+    barrier = pltpu.get_barrier_semaphore()
+
+    def greet(s):
+        toward = 1 - 2 * s
+        for step in ((1, 0, 0), (0, 1, 0), (0, -1, 0), (1, -toward, 0), (0, 0, 1), (0, 0, -1)):
+            pl.semaphore_signal(barrier, inc=1, device_id=device(*step), device_id_type=MESH)
+
+    by_side(greet)
+
+    own_planes, far_planes = pl.ds(0, nx), pl.ds(nx, nx)
+
+    def own_rows(s):
+        if s == 0:
+            return pl.ds(0, half + REACH), pl.ds(ROWS + REACH, half + REACH)
+        return pl.ds(half - REACH, half + REACH), pl.ds(ROWS, half + REACH)
+
+    def loads(s):
+        box, place_in = own_rows(s)
+        return [
+            pltpu.make_async_copy(bits, bit_box, load_sem.at[0]),
+            pltpu.make_async_copy(flag, flag_box, load_sem.at[1]),
+            pltpu.make_async_copy(fields.at[:, :, box], raw.at[:, own_planes, place_in], load_sem.at[2]),
+            pltpu.make_async_copy(code.at[:, box], rawcode.at[own_planes, place_in], load_sem.at[3]),
+        ]
+
+    def remote(src, dst, send, recv, step):
+        return pltpu.make_async_remote_copy(
+            src_ref=src, dst_ref=dst, send_sem=send, recv_sem=recv,
+            device_id=device(*step), device_id_type=MESH,
+        )
+
+    def triple(from_rows, to_planes, to_rows, send, recv, step):
+        return [
+            remote(fields.at[:, :, from_rows], raw.at[:, to_planes, to_rows], send.at[0], recv.at[0], step),
+            remote(code.at[:, from_rows], rawcode.at[to_planes, to_rows], send.at[1], recv.at[1], step),
+            remote(act_box.at[:, from_rows], act.at[0, to_planes, to_rows], send.at[2], recv.at[2], step),
+        ]
+
+    def x_rows(s, t):
+        if s == 0:
+            size = ROWS if t < tiles - 1 else ROWS - REACH
+            return pl.ds(half - REACH + ROWS * t, size), pl.ds(ROWS * (t + 1), size)
+        if t == 0:
+            return pl.ds(0, ROWS - REACH), pl.ds(ROWS + REACH, ROWS - REACH)
+        return pl.ds(ROWS * t - REACH, ROWS), pl.ds(ROWS * (t + 1), ROWS)
+
+    def x_copies(s, t):
+        from_rows, to_rows = x_rows(s, t)
+        return triple(from_rows, far_planes, to_rows, x_send.at[t], x_recv.at[t], (1, 0, 0))
+
+    def y_copies(s, cross):
+        low, high = pl.ds(0, REACH), pl.ds(last, REACH)
+        up = (s == 0) != cross
+        rows, to_rows = (high, pl.ds(top, REACH)) if up else (low, pl.ds(bottom, REACH))
+        to_planes = far_planes if cross else own_planes
+        step = (1 if cross else 0, 1 if up else -1, 0)
+        return triple(rows, to_planes, to_rows, y_send.at[int(cross)], y_recv.at[int(cross)], step)
+
+    def z_copies(t):
+        rows = pl.ds(ROWS * t, ROWS)
+        copies = []
+        for k, dz in enumerate((1, -1)):
+            copies.append(remote(
+                packed.at[:, rows], landed.at[k, :, rows], z_send.at[t, k, 0], z_recv.at[t, k, 0], (0, 0, dz),
+            ))
+            copies.append(remote(
+                act_packed.at[rows], act_landed.at[k, rows], z_send.at[t, k, 1], z_recv.at[t, k, 1], (0, 0, dz),
+            ))
+        return copies
+
+    def box_rows(s, k):
+        return pl.ds(pl.multiple_of(s * half + ROWS * k, ROWS), ROWS)
+
+    def back_copy(k):
+        return remote(
+            done.at[k, :, far_planes], out.at[:, :, box_rows(side, k)], back_send.at[k], back_recv.at[k], (1, 0, 0),
+        )
+
+    def own_copy(k):
+        return pltpu.make_async_copy(done.at[k, :, own_planes], out.at[:, :, box_rows(side, k)], own_sem.at[k])
+
+    lane = lax.broadcasted_iota(jnp.int32, (ROWS, nz), 1)
+    within = jnp.bitwise_and(lane, GROUP - 1)
+    member_of = jnp.right_shift(lane, GROUP.bit_length() - 1)
+
+    def rolled(value, amount):
+        amount %= nz
+        return pltpu.roll(value, amount, 1) if amount else value
+
+    def aligned(t):
+        return pl.ds(ROWS * (t + 1), ROWS)
+
+    def begin(s):
+        copies = loads(s)
+        for copy in copies:
+            copy.start()
+        for copy in copies[:2]:
+            copy.wait()
+        box, place_in = own_rows(s)
+
+        def plane(x, carry):
+            for j in range(ny // ROWS):
+                rows = pl.ds(ROWS * j, ROWS)
+                act_box[x, rows] = bit_box[x, rows] * flag_box[x, rows]
+            return carry
+
+        lax.fori_loop(0, nx, plane, 0)
+
+        pl.semaphore_wait(barrier, 6)
+        first, later = y_copies(s, False), y_copies(s, True)
+        copies = first + (later if s == 1 else [])
+        for t in range(tiles):
+            copies += x_copies(s, t)
+        for copy in copies + (later if s == 0 else []):
+            copy.start()
+
+        def keep(x, carry):
+            start, end, size = box.start, place_in.start, box.size
+            for j in range(0, size, ROWS):
+                n = min(ROWS, size - j)
+                act[0, x, pl.ds(end + j, n)] = act_box[x, pl.ds(start + j, n)]
+            return carry
+
+        lax.fori_loop(0, nx, keep, 0)
+        for copy in loads(s)[2:]:
+            copy.wait()
+
+    by_side(begin)
+
+    def arrived(s, t):
+        for copy in x_copies(1 - s, t):
+            copy.wait_recv()
+        if t == (tiles - 1) * s:
+            for copy in y_copies(s, False) + y_copies(1 - s, True):
+                copy.wait_recv()
+
+    def prepare(t):
+        rows = aligned(t)
+
+        def plane(x, carry):
+            kappa = rawcode[x, rows].astype(jnp.float32) * (1.0 / 1048576.0)
+            pull0[0, 0, x, rows] = kappa
+            for c in range(nf):
+                pull0[0, c + 1, x, rows] = kappa * raw[c, x, rows]
+            others = ones_in(jnp.bitwise_and(act[0, x, rows], ((1 << 27) - 1) ^ (1 << 13)))
+            scale = 1.0 / (1 + others).astype(jnp.float32)
+            inverse[x, rows] = scale
+            weight[x, rows] = scale * kappa
+            return carry
+
+        lax.fori_loop(0, planes, plane, 0)
+        to = pl.ds(ROWS * t, ROWS)
+        for c in range(-1, nf + 1):
+            tile = None
+            for x in range(planes):
+                value = act[0, x, rows] if c < 0 else pull0[0, c, x, rows]
+                value = rolled(value, GROUP * x + 2 * REACH)
+                tile = value if tile is None else jnp.where(member_of == x, value, tile)
+            if c < 0:
+                act_packed[to] = tile
+            else:
+                packed[c, to] = tile
+        for copy in z_copies(t):
+            copy.start()
+
+    turns = [(sx, sz) for sx in (-1, 0, 1) for sz in (-1, 0, 1)]
+
+    def spread(tile, keep, keep_end):
+        for v, (sx, sz) in enumerate(turns):
+            keep(v, rolled(tile, -(GROUP * sx + sz)))
+        for x in range(planes):
+            low = rolled(tile, -(GROUP * x + REACH - 1))
+            high = rolled(tile, nz - 1 - (GROUP * x + 3 * REACH))
+            keep_end(x, jnp.where(lane == 0, low, high))
+
+    def beside(value, end):
+        return (
+            jnp.where(lane == 0, end, rolled(value, 1)),
+            jnp.where(lane == nz - 1, end, rolled(value, -1)),
+        )
+
+    def unpack(t):
+        for copy in z_copies(t):
+            copy.wait_recv()
+        rows, at = aligned(t), pl.ds(ROWS * t, ROWS)
+
+        def joined(own, low, high):
+            left = rolled(jnp.where(within < 2 * REACH, low, own), -REACH)
+            right = rolled(jnp.where(within < 2 * REACH, own, high), REACH)
+            return jnp.where(within < 2 * REACH, left, right)
+
+        tile = joined(act_packed[at], act_landed[0, at], act_landed[1, at])
+
+        def keep(v, value):
+            edge_act[v, rows] = value
+
+        def keep_end(x, value):
+            act_ends[x] = value
+
+        spread(tile, keep, keep_end)
+        others = ones_in(jnp.bitwise_and(tile, ((1 << 27) - 1) ^ (1 << 13)))
+        scale = 1.0 / (1 + others).astype(jnp.float32)
+        for c in range(nf + 1):
+            tile = joined(packed[c, at], landed[0, c, at], landed[1, c, at])
+            if c == 0:
+                edge_weight[rows] = scale * tile
+
+            def keep(v, value):
+                edge0[v, c, rows] = value
+
+            def keep_end(x, value):
+                ends[c, x] = value
+
+            spread(tile, keep, keep_end)
+
+        def plane(x, carry):
+            low, high = beside(act[0, x, rows], act_ends[x])
+            act[1, x, rows], act[2, x, rows] = low, high
+            for c in range(nf + 1):
+                low, high = beside(pull0[0, c, x, rows], ends[c, x])
+                pull0[1, c, x, rows], pull0[2, c, x, rows] = low, high
+            return carry
+
+        lax.fori_loop(0, planes, plane, 0, unroll=2)
+
+    def gathered(mask_at, value_at, arrays, pulls):
+        values = list(value_at(0, 0, 0))
+        center = None if pulls else mask_at(0, 0, 0)
+        for sx in (-1, 0, 1):
+            for sy in (-1, 0, 1):
+                for sz in (-1, 0, 1):
+                    if (sx, sy, sz) == (0, 0, 0):
+                        continue
+                    if pulls:
+                        member = bit_of(mask_at(sx, sy, sz), -sx, -sy, -sz)
+                    else:
+                        member = bit_of(center, sx, sy, sz)
+                    terms = value_at(sx, sy, sz)
+                    values = [a + jnp.where(member, b, 0.0) for a, b in zip(values, terms)]
+        return values
+
+    shifts = {0: 0, -1: 1, 1: 2}
+
+    def edge_values(source, arrays, pulls, first):
+        def rows(sy):
+            return pl.ds(first + sy, ROWS)
+
+        def mask_at(sx, sy, sz):
+            return edge_act[turns.index((sx, sz)), rows(sy)]
+
+        def value_at(sx, sy, sz):
+            return [source[turns.index((sx, sz)), c, rows(sy)] for c in range(arrays)]
+
+        return gathered(mask_at, value_at, arrays, pulls)
+
+    def plane_values(source, arrays, pulls, first, x):
+        at = {0: x, -1: jnp.where(x == 0, planes - 1, x - 1), 1: jnp.where(x == planes - 1, 0, x + 1)}
+
+        def rows(sy):
+            return pl.ds(first + sy, ROWS)
+
+        def mask_at(sx, sy, sz):
+            return act[shifts[sz], at[sx], rows(sy)]
+
+        def value_at(sx, sy, sz):
+            return [source[shifts[sz], c, at[sx], rows(sy)] for c in range(arrays)]
+
+        return gathered(mask_at, value_at, arrays, pulls)
+
+    def finish(values, stage, read_weight, read_volume, write_volume):
+        if stage == 0:
+            scale = 1.0 / values[0]
+            write_volume(scale)
+            values = values[1:]
+        elif stage == 1:
+            scale = read_weight()
+        else:
+            scale = read_volume()
+        return [value * scale for value in values]
+
+    sources = ((pull0, edge0), (push0, edge1), (pull1, edge2), (push1, edge3))
+
+    def advance(stage, t):
+        rows = aligned(t)
+        first = ROWS * (t + 1)
+        source, edge_source = sources[stage]
+        target, edge_target = sources[stage + 1]
+        arrays = nf + 1 if stage == 0 else nf
+        pulls = stage % 2 == 0
+
+        def write_edge_volume(value):
+            edge_volume[rows] = value
+
+        values = edge_values(edge_source, arrays, pulls, first)
+        values = finish(
+            values, stage, lambda: edge_weight[rows], lambda: edge_volume[rows], write_edge_volume
+        )
+        for c, value in enumerate(values):
+            def keep(v, moved):
+                edge_target[v, c, rows] = moved
+
+            def keep_end(x, moved):
+                ends[c, x] = moved
+
+            spread(value, keep, keep_end)
+
+        def plane(x, carry):
+            def write_volume(value):
+                volume[x, rows] = value
+
+            values = plane_values(source, arrays, pulls, first, x)
+            values = finish(values, stage, lambda: weight[x, rows], lambda: volume[x, rows], write_volume)
+            for c, value in enumerate(values):
+                low, high = beside(value, ends[c, x])
+                target[0, c, x, rows] = value
+                target[1, c, x, rows] = low
+                target[2, c, x, rows] = high
+            return carry
+
+        lax.fori_loop(0, planes, plane, 0, unroll=2)
+
+    def deliver(k):
+        first = ROWS + REACH + ROWS * k
+
+        def plane(x, carry):
+            scale = inverse[x, pl.ds(first, ROWS)]
+            for c, value in enumerate(plane_values(push1, nf, False, first, x)):
+                done[k, c, x] = value * scale
+            return carry
+
+        lax.fori_loop(0, planes, plane, 0, unroll=2)
+        back_copy(k).start()
+        own_copy(k).start()
+
+    for u in range(tiles + 4):
+        if u < tiles:
+            by_side(functools.partial(lambda t, s: arrived(s, t), u))
+            prepare(u)
+        if 0 <= u - 1 < tiles:
+            unpack(u - 1)
+        for stage in range(3):
+            if 0 <= u - 2 - stage < tiles:
+                advance(stage, u - 2 - stage)
+        if 0 <= u - 5:
+            deliver(u - 5)
+
+    for t in range(tiles):
+        for copy in z_copies(t):
+            copy.wait_send()
+
+    def drain(s):
+        for copy in y_copies(s, False) + y_copies(s, True):
+            copy.wait_send()
+        for t in range(tiles):
+            for copy in x_copies(s, t):
+                copy.wait_send()
+
+    by_side(drain)
+    for k in range(tiles - 1):
+        own_copy(k).wait()
+        back_copy(k).wait()
+
+
+def folded_body(counts, fields, code, flag, bits):
+    nf, nx, ny, nz = fields.shape
+    planes = 2 * nx
+    depth = ny // 2 + 2 * REACH
+    tiles = depth // ROWS
+    high = depth + 2 * ROWS
+    f32, i32 = jnp.float32, jnp.int32
+    whole = pl.BlockSpec(memory_space=pl.ANY)
+    dma = pltpu.SemaphoreType.DMA
+
+    def main(n):
+        return pltpu.VMEM((3, n, planes, high, nz), f32)
+
+    def edge(n):
+        return pltpu.VMEM((9, n, high, nz), f32)
+
+    return pl.pallas_call(
+        functools.partial(folded_kernel, counts),
+        out_shape=jax.ShapeDtypeStruct(fields.shape, f32),
+        in_specs=[whole] * 4,
+        out_specs=whole,
+        scratch_shapes=[
+            pltpu.VMEM((nf, planes, high, nz), f32),
+            pltpu.VMEM((planes, high, nz), i32),
+            pltpu.VMEM((nx, ny, nz), i32),
+            pltpu.VMEM((nx, ny, nz), i32),
+            pltpu.VMEM((nx, ny, nz), i32),
+            pltpu.VMEM((3, planes, high, nz), i32),
+            main(nf + 1), main(nf), main(nf), main(nf),
+            pltpu.VMEM((9, high, nz), i32),
+            edge(nf + 1), edge(nf), edge(nf), edge(nf),
+            pltpu.VMEM((nf + 1, planes, ROWS, nz), f32),
+            pltpu.VMEM((planes, ROWS, nz), i32),
+            pltpu.VMEM((planes, high, nz), f32),
+            pltpu.VMEM((planes, high, nz), f32),
+            pltpu.VMEM((planes, high, nz), f32),
+            pltpu.VMEM((high, nz), f32),
+            pltpu.VMEM((high, nz), f32),
+            pltpu.VMEM((nf + 1, depth, nz), f32),
+            pltpu.VMEM((depth, nz), i32),
+            pltpu.VMEM((2, nf + 1, depth, nz), f32),
+            pltpu.VMEM((2, depth, nz), i32),
+            pltpu.VMEM((tiles - 1, nf, planes, ROWS, nz), f32),
+            dma((4,)),
+            dma((tiles, 3)), dma((tiles, 3)),
+            dma((2, 3)), dma((2, 3)),
+            dma((tiles, 2, 2)), dma((tiles, 2, 2)),
+            dma((tiles - 1,)), dma((tiles - 1,)), dma((tiles - 1,)),
+        ],
+        compiler_params=pltpu.CompilerParams(collective_id=0, has_side_effects=True),
+    )(fields, code, flag, bits)
+
+
+def any_body(counts, fields, code, flag, bits):
+    nf, nx, ny, nz = fields.shape
+    folds = (
+        counts[0] == 2 and min(counts) > 1
+        and 2 * nx * GROUP == nz
+        and ny % (2 * ROWS) == 0 and ny // 2 >= REACH and 2 * REACH == ROWS
+    )
+    return (folded_body if folds else body)(counts, fields, code, flag, bits)
+
+
 def solution(mesh):
     counts = tuple(mesh.shape[name] for name in AXES)
     spec = P("gx", "gy", "gz")
     whole = P(None, "gx", "gy", "gz")
     return jax.shard_map(
-        functools.partial(body, counts),
+        functools.partial(any_body, counts),
         mesh=mesh,
         in_specs=(whole, spec, spec, spec),
         out_specs=whole,

time: 59.3 us -> 42.9 us (0.72)
  Pallas kernels: 57.2 us -> 40.8 us
    pallas_call x1, Pallas kernels: 57.2 us -> 40.8 us  [folded_body(): pl.pallas_call(functools.partial(folded_kernel, counts), out_shape=jax.Sh...]
where the time goes in v1:
time: 42.9 us; the launch traced here: 42.7 us
  Pallas kernels  40.8 us (95%)
  local copies, waits for them, and re-layouts  1.89 us (4%)
    pallas_call x1, Pallas kernels, folded_body(): pl.pallas_call(functools.partial(folded_kernel, counts), out_shape=jax.Sh...  40.8 us
    unnamed x1, local copies, waits for them, and re-layouts  1.89 us

profile of v1, /device:TPU:0, one launch (start us, length us, event | category | flops | bytes accessed | tf_op | source)
XLA Modules:
  0.0 42.7 jit_solution(16577359000435794265)
XLA Ops:
  0.0 40.8 %shard_map.46 = f32[4,4,64,128]{3,2,1,0:T(8,128)} custom-call(f32[4,4,64,128]{3,2,1,0:T(8,128)} %fields.1, s32[4,64,128]{2,1,0:T(8,128)} %code.1, s32[4,64,128]{2,1,0:T(8,128)} %flag.1, s32[4,64,128]{2,1,0:T(8,128)} %bits.1), custom_call_target="tpu_custom_call" | custom-call | tf_op jit(solution)/shard_map/pallas_call | solution.py:808
  40.8 1.9 %copy.6 = f32[4,4,64,128]{3,2,1,0:T(8,128)} copy(f32[4,4,64,128]{3,2,1,0:T(8,128)} %shard_map.46) | data formatting | bytes 1048576

commit v2 on v1

--- a/solution.py
+++ b/solution.py
@@ -485,7 +485,7 @@
         return triple(rows, to_planes, to_rows, y_send.at[int(cross)], y_recv.at[int(cross)], step)
 
     def z_copies(t):
-        rows = pl.ds(ROWS * t, ROWS)
+        rows = pl.ds(pl.multiple_of(ROWS * t, ROWS), ROWS)
         copies = []
         for k, dz in enumerate((1, -1)):
             copies.append(remote(
@@ -515,9 +515,6 @@
         amount %= nz
         return pltpu.roll(value, amount, 1) if amount else value
 
-    def aligned(t):
-        return pl.ds(ROWS * (t + 1), ROWS)
-
     def begin(s):
         copies = loads(s)
         for copy in copies:
@@ -555,39 +552,62 @@
 
     by_side(begin)
 
-    def arrived(s, t):
-        for copy in x_copies(1 - s, t):
-            copy.wait_recv()
-        if t == (tiles - 1) * s:
-            for copy in y_copies(s, False) + y_copies(1 - s, True):
+    def arrived(t):
+        short = t == (tiles - 1) * side
+
+        def wait_rows(size):
+            rows = pl.ds(0, size)
+            for copy in triple(rows, far_planes, rows, x_send.at[t], x_recv.at[t], (1, 0, 0)):
                 copy.wait_recv()
 
+        @pl.when(short)
+        def _():
+            wait_rows(ROWS - REACH)
+            for cross in (False, True):
+                for copy in y_copies(0, cross):
+                    copy.wait_recv()
+
+        @pl.when(jnp.logical_not(short))
+        def _():
+            wait_rows(ROWS)
+
+    def view(ref, t, *lead):
+        return ref.at[(*lead, pl.ds(pl.multiple_of(ROWS * t, ROWS), 3 * ROWS))]
+
+    def get(ref, t, offset, *lead):
+        return view(ref, t, *lead)[pl.ds(offset, ROWS)]
+
+    def put(ref, t, offset, *lead):
+        def write(value):
+            view(ref, t, *lead)[pl.ds(offset, ROWS)] = value
+        return write
+
+    def strip(t):
+        return pl.ds(pl.multiple_of(ROWS * t, ROWS), ROWS)
+
     def prepare(t):
-        rows = aligned(t)
-
         def plane(x, carry):
-            kappa = rawcode[x, rows].astype(jnp.float32) * (1.0 / 1048576.0)
-            pull0[0, 0, x, rows] = kappa
+            kappa = get(rawcode, t, ROWS, x).astype(jnp.float32) * (1.0 / 1048576.0)
+            put(pull0, t, ROWS, 0, x, 0)(kappa)
             for c in range(nf):
-                pull0[0, c + 1, x, rows] = kappa * raw[c, x, rows]
-            others = ones_in(jnp.bitwise_and(act[0, x, rows], ((1 << 27) - 1) ^ (1 << 13)))
+                put(pull0, t, ROWS, 0, x, c + 1)(kappa * get(raw, t, ROWS, c, x))
+            others = ones_in(jnp.bitwise_and(get(act, t, ROWS, 0, x), ((1 << 27) - 1) ^ (1 << 13)))
             scale = 1.0 / (1 + others).astype(jnp.float32)
-            inverse[x, rows] = scale
-            weight[x, rows] = scale * kappa
+            put(inverse, t, ROWS, x)(scale)
+            put(weight, t, ROWS, x)(scale * kappa)
             return carry
 
-        lax.fori_loop(0, planes, plane, 0)
-        to = pl.ds(ROWS * t, ROWS)
+        lax.fori_loop(0, planes, plane, 0, unroll=8)
         for c in range(-1, nf + 1):
             tile = None
             for x in range(planes):
-                value = act[0, x, rows] if c < 0 else pull0[0, c, x, rows]
+                value = get(act, t, ROWS, 0, x) if c < 0 else get(pull0, t, ROWS, 0, x, c)
                 value = rolled(value, GROUP * x + 2 * REACH)
                 tile = value if tile is None else jnp.where(member_of == x, value, tile)
             if c < 0:
-                act_packed[to] = tile
+                act_packed[strip(t)] = tile
             else:
-                packed[c, to] = tile
+                packed[c, strip(t)] = tile
         for copy in z_copies(t):
             copy.start()
 
@@ -595,11 +615,11 @@
 
     def spread(tile, keep, keep_end):
         for v, (sx, sz) in enumerate(turns):
-            keep(v, rolled(tile, -(GROUP * sx + sz)))
+            keep(v)(rolled(tile, -(GROUP * sx + sz)))
+        meet = 3 * REACH + 1
+        pair = jnp.where(within == meet, rolled(tile, meet - (REACH - 1)), tile)
         for x in range(planes):
-            low = rolled(tile, -(GROUP * x + REACH - 1))
-            high = rolled(tile, nz - 1 - (GROUP * x + 3 * REACH))
-            keep_end(x, jnp.where(lane == 0, low, high))
+            keep_end(x, rolled(pair, -(GROUP * x + meet)))
 
     def beside(value, end):
         return (
@@ -610,7 +630,7 @@
     def unpack(t):
         for copy in z_copies(t):
             copy.wait_recv()
-        rows, at = aligned(t), pl.ds(ROWS * t, ROWS)
+        at = strip(t)
 
         def joined(own, low, high):
             left = rolled(jnp.where(within < 2 * REACH, low, own), -REACH)
@@ -619,37 +639,33 @@
 
         tile = joined(act_packed[at], act_landed[0, at], act_landed[1, at])
 
-        def keep(v, value):
-            edge_act[v, rows] = value
-
         def keep_end(x, value):
             act_ends[x] = value
 
-        spread(tile, keep, keep_end)
+        spread(tile, lambda v: put(edge_act, t, ROWS, v), keep_end)
         others = ones_in(jnp.bitwise_and(tile, ((1 << 27) - 1) ^ (1 << 13)))
         scale = 1.0 / (1 + others).astype(jnp.float32)
         for c in range(nf + 1):
             tile = joined(packed[c, at], landed[0, c, at], landed[1, c, at])
             if c == 0:
-                edge_weight[rows] = scale * tile
-
-            def keep(v, value):
-                edge0[v, c, rows] = value
+                put(edge_weight, t, ROWS)(scale * tile)
 
             def keep_end(x, value):
-                ends[c, x] = value
-
-            spread(tile, keep, keep_end)
+                ends[x, c] = value
+
+            spread(tile, lambda v: put(edge0, t, ROWS, v, c), keep_end)
 
         def plane(x, carry):
-            low, high = beside(act[0, x, rows], act_ends[x])
-            act[1, x, rows], act[2, x, rows] = low, high
+            low, high = beside(get(act, t, ROWS, 0, x), act_ends[x])
+            put(act, t, ROWS, 1, x)(low)
+            put(act, t, ROWS, 2, x)(high)
             for c in range(nf + 1):
-                low, high = beside(pull0[0, c, x, rows], ends[c, x])
-                pull0[1, c, x, rows], pull0[2, c, x, rows] = low, high
+                low, high = beside(get(pull0, t, ROWS, 0, x, c), ends[x, c])
+                put(pull0, t, ROWS, 1, x, c)(low)
+                put(pull0, t, ROWS, 2, x, c)(high)
             return carry
 
-        lax.fori_loop(0, planes, plane, 0, unroll=2)
+        lax.fori_loop(0, planes, plane, 0, unroll=8)
 
     def gathered(mask_at, value_at, arrays, pulls):
         values = list(value_at(0, 0, 0))
@@ -669,29 +685,23 @@
 
     shifts = {0: 0, -1: 1, 1: 2}
 
-    def edge_values(source, arrays, pulls, first):
-        def rows(sy):
-            return pl.ds(first + sy, ROWS)
-
+    def edge_values(source, arrays, pulls, t, first):
         def mask_at(sx, sy, sz):
-            return edge_act[turns.index((sx, sz)), rows(sy)]
+            return get(edge_act, t, first + sy, turns.index((sx, sz)))
 
         def value_at(sx, sy, sz):
-            return [source[turns.index((sx, sz)), c, rows(sy)] for c in range(arrays)]
+            return [get(source, t, first + sy, turns.index((sx, sz)), c) for c in range(arrays)]
 
         return gathered(mask_at, value_at, arrays, pulls)
 
-    def plane_values(source, arrays, pulls, first, x):
+    def plane_values(source, arrays, pulls, t, first, x):
         at = {0: x, -1: jnp.where(x == 0, planes - 1, x - 1), 1: jnp.where(x == planes - 1, 0, x + 1)}
 
-        def rows(sy):
-            return pl.ds(first + sy, ROWS)
-
         def mask_at(sx, sy, sz):
-            return act[shifts[sz], at[sx], rows(sy)]
+            return get(act, t, first + sy, shifts[sz], at[sx])
 
         def value_at(sx, sy, sz):
-            return [source[shifts[sz], c, at[sx], rows(sy)] for c in range(arrays)]
+            return [get(source, t, first + sy, shifts[sz], at[sx], c) for c in range(arrays)]
 
         return gathered(mask_at, value_at, arrays, pulls)
 
@@ -709,68 +719,70 @@
     sources = ((pull0, edge0), (push0, edge1), (pull1, edge2), (push1, edge3))
 
     def advance(stage, t):
-        rows = aligned(t)
-        first = ROWS * (t + 1)
+        first = ROWS - 1 - stage
         source, edge_source = sources[stage]
         target, edge_target = sources[stage + 1]
         arrays = nf + 1 if stage == 0 else nf
         pulls = stage % 2 == 0
-
-        def write_edge_volume(value):
-            edge_volume[rows] = value
-
-        values = edge_values(edge_source, arrays, pulls, first)
+        values = edge_values(edge_source, arrays, pulls, t, first)
         values = finish(
-            values, stage, lambda: edge_weight[rows], lambda: edge_volume[rows], write_edge_volume
+            values, stage, lambda: get(edge_weight, t, first),
+            lambda: get(edge_volume, t, first), put(edge_volume, t, first),
         )
         for c, value in enumerate(values):
-            def keep(v, moved):
-                edge_target[v, c, rows] = moved
-
             def keep_end(x, moved):
-                ends[c, x] = moved
-
-            spread(value, keep, keep_end)
+                ends[x, c] = moved
+
+            spread(value, lambda v: put(edge_target, t, first, v, c), keep_end)
 
         def plane(x, carry):
-            def write_volume(value):
-                volume[x, rows] = value
-
-            values = plane_values(source, arrays, pulls, first, x)
-            values = finish(values, stage, lambda: weight[x, rows], lambda: volume[x, rows], write_volume)
+            values = plane_values(source, arrays, pulls, t, first, x)
+            values = finish(
+                values, stage, lambda: get(weight, t, first, x),
+                lambda: get(volume, t, first, x), put(volume, t, first, x),
+            )
             for c, value in enumerate(values):
-                low, high = beside(value, ends[c, x])
-                target[0, c, x, rows] = value
-                target[1, c, x, rows] = low
-                target[2, c, x, rows] = high
+                low, high = beside(value, ends[x, c])
+                put(target, t, first, 0, x, c)(value)
+                put(target, t, first, 1, x, c)(low)
+                put(target, t, first, 2, x, c)(high)
             return carry
 
-        lax.fori_loop(0, planes, plane, 0, unroll=2)
-
-    def deliver(k):
-        first = ROWS + REACH + ROWS * k
+        lax.fori_loop(0, planes, plane, 0, unroll=8)
+
+    def deliver(t):
+        k = t - 1
+        first = REACH
 
         def plane(x, carry):
-            scale = inverse[x, pl.ds(first, ROWS)]
-            for c, value in enumerate(plane_values(push1, nf, False, first, x)):
+            scale = get(inverse, t, first, x)
+            for c, value in enumerate(plane_values(push1, nf, False, t, first, x)):
                 done[k, c, x] = value * scale
             return carry
 
-        lax.fori_loop(0, planes, plane, 0, unroll=2)
+        lax.fori_loop(0, planes, plane, 0, unroll=8)
         back_copy(k).start()
         own_copy(k).start()
 
-    for u in range(tiles + 4):
-        if u < tiles:
-            by_side(functools.partial(lambda t, s: arrived(s, t), u))
+    def step(u, carry):
+        @pl.when(u < tiles)
+        def _():
+            arrived(u)
             prepare(u)
-        if 0 <= u - 1 < tiles:
+
+        @pl.when(u > 0)
+        def _():
             unpack(u - 1)
-        for stage in range(3):
-            if 0 <= u - 2 - stage < tiles:
-                advance(stage, u - 2 - stage)
-        if 0 <= u - 5:
-            deliver(u - 5)
+            for stage in range(3):
+                advance(stage, u - 1)
+
+        @pl.when(u > 1)
+        def _():
+            deliver(u - 1)
+
+        return carry
+
+    lax.fori_loop(0, tiles + 1, step, 0)
 
     for t in range(tiles):
         for copy in z_copies(t):
@@ -800,7 +812,7 @@
     dma = pltpu.SemaphoreType.DMA
 
     def main(n):
-        return pltpu.VMEM((3, n, planes, high, nz), f32)
+        return pltpu.VMEM((3, planes, n, high, nz), f32)
 
     def edge(n):
         return pltpu.VMEM((9, n, high, nz), f32)
@@ -820,7 +832,7 @@
             main(nf + 1), main(nf), main(nf), main(nf),
             pltpu.VMEM((9, high, nz), i32),
             edge(nf + 1), edge(nf), edge(nf), edge(nf),
-            pltpu.VMEM((nf + 1, planes, ROWS, nz), f32),
+            pltpu.VMEM((planes, nf + 1, ROWS, nz), f32),
             pltpu.VMEM((planes, ROWS, nz), i32),
             pltpu.VMEM((planes, high, nz), f32),
             pltpu.VMEM((planes, high, nz), f32),

time: 42.9 us -> 32.6 us (0.76)
  Pallas kernels: 40.8 us -> 30.5 us
    pallas_call x1, Pallas kernels: 40.8 us -> 30.5 us  [folded_body(): pl.pallas_call(functools.partial(folded_kernel, counts), out_shape=jax.Sh...]
where the time goes in v2:
time: 32.6 us; the launch traced here: 32.4 us
  Pallas kernels  30.5 us (94%)
  local copies, waits for them, and re-layouts  1.89 us (6%)
    pallas_call x1, Pallas kernels, folded_body(): pl.pallas_call(functools.partial(folded_kernel, counts), out_shape=jax.Sh...  30.5 us
    unnamed x1, local copies, waits for them, and re-layouts  1.89 us

profile of v2, /device:TPU:0, one launch (start us, length us, event | category | flops | bytes accessed | tf_op | source)
XLA Modules:
  0.0 32.4 jit_solution(16224682267222399761)
XLA Ops:
  0.0 30.5 %shard_map.46 = f32[4,4,64,128]{3,2,1,0:T(8,128)} custom-call(f32[4,4,64,128]{3,2,1,0:T(8,128)} %fields.1, s32[4,64,128]{2,1,0:T(8,128)} %code.1, s32[4,64,128]{2,1,0:T(8,128)} %flag.1, s32[4,64,128]{2,1,0:T(8,128)} %bits.1), custom_call_target="tpu_custom_call" | custom-call | tf_op jit(solution)/shard_map/pallas_call | solution.py:820
  30.5 1.9 %copy.6 = f32[4,4,64,128]{3,2,1,0:T(8,128)} copy(f32[4,4,64,128]{3,2,1,0:T(8,128)} %shard_map.46) | data formatting | bytes 1048576

commit v3 on v2

--- a/solution.py
+++ b/solution.py
@@ -402,7 +402,7 @@
     edge_act, edge0, edge1, edge2, edge3, ends, act_ends,
     volume, inverse, weight, edge_volume, edge_weight,
     packed, act_packed, landed, act_landed, done,
-    load_sem, x_send, x_recv, y_send, y_recv, z_send, z_recv, back_send, back_recv, own_sem,
+    load_sem, x_send, x_recv, y_send, y_recv, z_send, z_recv, back_send, back_recv, token,
 ):
     nf, nx, ny, nz = fields.shape
     planes = 2 * nx
@@ -428,12 +428,29 @@
 
     barrier = pltpu.get_barrier_semaphore()
 
-    def greet(s):
-        toward = 1 - 2 * s
-        for step in ((1, 0, 0), (0, 1, 0), (0, -1, 0), (1, -toward, 0), (0, 0, 1), (0, 0, -1)):
-            pl.semaphore_signal(barrier, inc=1, device_id=device(*step), device_id_type=MESH)
-
-    by_side(greet)
+    row, end_row = place[1], counts[1] - 1
+    near = [(1, 0, 0), (0, 0, 1), (0, 0, -1)]
+    not_first, not_last = row > 0, row < end_row
+
+    def tell(sem, step):
+        pl.semaphore_signal(sem, inc=1, device_id=device(*step), device_id_type=MESH)
+
+    for step in near:
+        tell(barrier, step)
+    for there, dy in ((not_first, -1), (not_last, 1)):
+        pl.when(there)(functools.partial(tell, barrier, (0, dy, 0)))
+
+    def meet_rows():
+        rising, falling, across = token.at[0], token.at[1], token.at[2]
+        pl.when(row == 0)(functools.partial(tell, rising, (0, 1, 0)))
+        pl.when(row == end_row)(functools.partial(tell, falling, (0, -1, 0)))
+        for sem, come, go, dy in ((rising, not_first, not_last, 1), (falling, not_last, not_first, -1)):
+            @pl.when(come)
+            def _(sem=sem, go=go, dy=dy):
+                pl.semaphore_wait(sem, 1)
+                pl.when(go)(functools.partial(tell, sem, (0, dy, 0)))
+        tell(across, (1, 0, 0))
+        pl.semaphore_wait(across, 1)
 
     own_planes, far_planes = pl.ds(0, nx), pl.ds(nx, nx)
 
@@ -471,6 +488,9 @@
         if t == 0:
             return pl.ds(0, ROWS - REACH), pl.ds(ROWS + REACH, ROWS - REACH)
         return pl.ds(ROWS * t - REACH, ROWS), pl.ds(ROWS * (t + 1), ROWS)
+
+    def order(s):
+        return range(tiles) if s == 1 else range(tiles - 1, -1, -1)
 
     def x_copies(s, t):
         from_rows, to_rows = x_rows(s, t)
@@ -500,12 +520,7 @@
         return pl.ds(pl.multiple_of(s * half + ROWS * k, ROWS), ROWS)
 
     def back_copy(k):
-        return remote(
-            done.at[k, :, far_planes], out.at[:, :, box_rows(side, k)], back_send.at[k], back_recv.at[k], (1, 0, 0),
-        )
-
-    def own_copy(k):
-        return pltpu.make_async_copy(done.at[k, :, own_planes], out.at[:, :, box_rows(side, k)], own_sem.at[k])
+        return remote(done.at[k], out.at[:, :, box_rows(side, k)], back_send.at[k], back_recv.at[k], (1, 0, 0))
 
     lane = lax.broadcasted_iota(jnp.int32, (ROWS, nz), 1)
     within = jnp.bitwise_and(lane, GROUP - 1)
@@ -519,9 +534,13 @@
         copies = loads(s)
         for copy in copies:
             copy.start()
+        box, place_in = own_rows(s)
+        chunks = [x_copies(s, t) for t in order(1 - s)]
+        pl.semaphore_wait(barrier, len(near) + not_first.astype(jnp.int32) + not_last.astype(jnp.int32))
+        for copy in chunks[0][:2]:
+            copy.start()
         for copy in copies[:2]:
             copy.wait()
-        box, place_in = own_rows(s)
 
         def plane(x, carry):
             for j in range(ny // ROWS):
@@ -529,14 +548,8 @@
                 act_box[x, rows] = bit_box[x, rows] * flag_box[x, rows]
             return carry
 
-        lax.fori_loop(0, nx, plane, 0)
-
-        pl.semaphore_wait(barrier, 6)
-        first, later = y_copies(s, False), y_copies(s, True)
-        copies = first + (later if s == 1 else [])
-        for t in range(tiles):
-            copies += x_copies(s, t)
-        for copy in copies + (later if s == 0 else []):
+        lax.fori_loop(0, nx, plane, 0, unroll=nx)
+        for copy in chunks[0][2:] + sum(chunks[1:], []):
             copy.start()
 
         def keep(x, carry):
@@ -546,14 +559,17 @@
                 act[0, x, pl.ds(end + j, n)] = act_box[x, pl.ds(start + j, n)]
             return carry
 
-        lax.fori_loop(0, nx, keep, 0)
-        for copy in loads(s)[2:]:
+        lax.fori_loop(0, nx, keep, 0, unroll=nx)
+        for copy in copies[2:]:
             copy.wait()
+        meet_rows()
+        for copy in y_copies(s, False) + y_copies(s, True):
+            copy.start()
 
     by_side(begin)
 
-    def arrived(t):
-        short = t == (tiles - 1) * side
+    def arrived(s, t):
+        short = t == (tiles - 1) * s
 
         def wait_rows(size):
             rows = pl.ds(0, size)
@@ -597,7 +613,7 @@
             put(weight, t, ROWS, x)(scale * kappa)
             return carry
 
-        lax.fori_loop(0, planes, plane, 0, unroll=8)
+        lax.fori_loop(0, planes, plane, 0, unroll=planes)
         for c in range(-1, nf + 1):
             tile = None
             for x in range(planes):
@@ -665,7 +681,7 @@
                 put(pull0, t, ROWS, 2, x, c)(high)
             return carry
 
-        lax.fori_loop(0, planes, plane, 0, unroll=8)
+        lax.fori_loop(0, planes, plane, 0, unroll=planes)
 
     def gathered(mask_at, value_at, arrays, pulls):
         values = list(value_at(0, 0, 0))
@@ -718,8 +734,8 @@
 
     sources = ((pull0, edge0), (push0, edge1), (pull1, edge2), (push1, edge3))
 
-    def advance(stage, t):
-        first = ROWS - 1 - stage
+    def advance(s, stage, t):
+        first = ROWS - 1 - stage if s == 1 else ROWS + 1 + stage
         source, edge_source = sources[stage]
         target, edge_target = sources[stage + 1]
         arrays = nf + 1 if stage == 0 else nf
@@ -748,41 +764,56 @@
                 put(target, t, first, 2, x, c)(high)
             return carry
 
-        lax.fori_loop(0, planes, plane, 0, unroll=8)
-
-    def deliver(t):
-        k = t - 1
-        first = REACH
-
-        def plane(x, carry):
+        lax.fori_loop(0, planes, plane, 0, unroll=planes)
+
+    def deliver(s, t):
+        k = t - s
+        first = REACH if s == 1 else ROWS + REACH
+        rows = box_rows(s, k)
+
+        def result(x):
             scale = get(inverse, t, first, x)
-            for c, value in enumerate(plane_values(push1, nf, False, t, first, x)):
-                done[k, c, x] = value * scale
+            return [value * scale for value in plane_values(push1, nf, False, t, first, x)]
+
+        def far(x, carry):
+            for c, value in enumerate(result(nx + x)):
+                done[k, c, x] = value
             return carry
 
-        lax.fori_loop(0, planes, plane, 0, unroll=8)
+        def near(x, carry):
+            for c, value in enumerate(result(x)):
+                out[c, x, rows] = value
+            return carry
+
+        lax.fori_loop(0, nx, far, 0, unroll=nx)
         back_copy(k).start()
-        own_copy(k).start()
-
-    def step(u, carry):
-        @pl.when(u < tiles)
-        def _():
-            arrived(u)
-            prepare(u)
-
-        @pl.when(u > 0)
-        def _():
-            unpack(u - 1)
-            for stage in range(3):
-                advance(stage, u - 1)
-
-        @pl.when(u > 1)
-        def _():
-            deliver(u - 1)
-
-        return carry
-
-    lax.fori_loop(0, tiles + 1, step, 0)
+        lax.fori_loop(0, nx, near, 0, unroll=nx)
+
+    def run(s):
+        def tile(u):
+            return u if s == 1 else tiles - 1 - u
+
+        def step(u, carry):
+            @pl.when(u < tiles)
+            def _():
+                arrived(s, tile(u))
+                prepare(tile(u))
+
+            @pl.when(u > 0)
+            def _():
+                unpack(tile(u - 1))
+                for stage in range(3):
+                    advance(s, stage, tile(u - 1))
+
+            @pl.when(u > 1)
+            def _():
+                deliver(s, tile(u - 1))
+
+            return carry
+
+        lax.fori_loop(0, tiles + 1, step, 0)
+
+    by_side(run)
 
     for t in range(tiles):
         for copy in z_copies(t):
@@ -797,7 +828,6 @@
 
     by_side(drain)
     for k in range(tiles - 1):
-        own_copy(k).wait()
         back_copy(k).wait()
 
 
@@ -819,9 +849,9 @@
 
     return pl.pallas_call(
         functools.partial(folded_kernel, counts),
-        out_shape=jax.ShapeDtypeStruct(fields.shape, f32),
+        out_shape=pltpu.VMEM(fields.shape, f32),
         in_specs=[whole] * 4,
-        out_specs=whole,
+        out_specs=pl.BlockSpec(memory_space=pltpu.VMEM),
         scratch_shapes=[
             pltpu.VMEM((nf, planes, high, nz), f32),
             pltpu.VMEM((planes, high, nz), i32),
@@ -843,12 +873,13 @@
             pltpu.VMEM((depth, nz), i32),
             pltpu.VMEM((2, nf + 1, depth, nz), f32),
             pltpu.VMEM((2, depth, nz), i32),
-            pltpu.VMEM((tiles - 1, nf, planes, ROWS, nz), f32),
+            pltpu.VMEM((tiles - 1, nf, nx, ROWS, nz), f32),
             dma((4,)),
             dma((tiles, 3)), dma((tiles, 3)),
             dma((2, 3)), dma((2, 3)),
             dma((tiles, 2, 2)), dma((tiles, 2, 2)),
-            dma((tiles - 1,)), dma((tiles - 1,)), dma((tiles - 1,)),
+            dma((tiles - 1,)), dma((tiles - 1,)),
+            pltpu.SemaphoreType.REGULAR((3,)),
         ],
         compiler_params=pltpu.CompilerParams(collective_id=0, has_side_effects=True),
     )(fields, code, flag, bits)

time: 32.6 us -> 28.9 us (0.89)
  Pallas kernels: 30.5 us -> 28 us
  local copies, waits for them, and re-layouts: 1.89 us -> 0.8 us
    pallas_call x1, Pallas kernels: 30.5 us -> 28 us  [folded_body(): pl.pallas_call(functools.partial(folded_kernel, counts), out_shape=pltpu....]
    unnamed x1, local copies, waits for them, and re-layouts: 1.89 us -> 0.8 us
where the time goes in v3:
time: 28.9 us; the launch traced here: 28.8 us
  Pallas kernels  28 us (97%)
  local copies, waits for them, and re-layouts  0.8 us (3%)
    pallas_call x1, Pallas kernels, folded_body(): pl.pallas_call(functools.partial(folded_kernel, counts), out_shape=pltpu....  28 us
    unnamed x1, local copies, waits for them, and re-layouts  0.8 us

profile of v3, /device:TPU:0, one launch (start us, length us, event | category | flops | bytes accessed | tf_op | source)
XLA Modules:
  0.0 28.8 jit_solution(9811498291654731342)
XLA Ops:
  0.0 28.0 %shard_map.46 = f32[4,4,64,128]{3,2,1,0:T(8,128)S(1)} custom-call(f32[4,4,64,128]{3,2,1,0:T(8,128)} %fields.1, s32[4,64,128]{2,1,0:T(8,128)} %code.1, s32[4,64,128]{2,1,0:T(8,128)} %flag.1, s32[4,64,128]{2,1,0:T(8,128)} %bits.1), custom_call_target="tpu_custom_call" | custom-call | tf_op jit(solution)/shard_map/pallas_call | solution.py:850
  28.0 0.8 %copy.6 = f32[4,4,64,128]{3,2,1,0:T(8,128)} copy(f32[4,4,64,128]{3,2,1,0:T(8,128)S(1)} %shard_map.46) | data formatting | bytes 1048576

commit v4 on v3

--- a/solution.py
+++ b/solution.py
@@ -398,7 +398,7 @@
 
 def folded_kernel(
     counts, fields, code, flag, bits, out,
-    raw, rawcode, bit_box, flag_box, act_box, act, pull0, push0, pull1, push1,
+    field_box, code_box, raw, rawcode, bit_box, flag_box, act_box, act, pull0, push0, pull1, push1,
     edge_act, edge0, edge1, edge2, edge3, ends, act_ends,
     volume, inverse, weight, edge_volume, edge_weight,
     packed, act_packed, landed, act_landed, done,
@@ -440,17 +440,16 @@
     for there, dy in ((not_first, -1), (not_last, 1)):
         pl.when(there)(functools.partial(tell, barrier, (0, dy, 0)))
 
-    def meet_rows():
-        rising, falling, across = token.at[0], token.at[1], token.at[2]
-        pl.when(row == 0)(functools.partial(tell, rising, (0, 1, 0)))
-        pl.when(row == end_row)(functools.partial(tell, falling, (0, -1, 0)))
-        for sem, come, go, dy in ((rising, not_first, not_last, 1), (falling, not_last, not_first, -1)):
-            @pl.when(come)
-            def _(sem=sem, go=go, dy=dy):
-                pl.semaphore_wait(sem, 1)
-                pl.when(go)(functools.partial(tell, sem, (0, dy, 0)))
-        tell(across, (1, 0, 0))
-        pl.semaphore_wait(across, 1)
+    rising, falling, across = token.at[0], token.at[1], token.at[2]
+
+    def pass_tokens(hop):
+        for sem, first, dy in ((rising, 0, 1), (falling, end_row, -1)):
+            @pl.when(row == first + dy * hop)
+            def _(sem=sem, dy=dy):
+                if hop > 0:
+                    pl.semaphore_wait(sem, 1)
+                if hop < counts[1] - 1:
+                    tell(sem, (0, dy, 0))
 
     own_planes, far_planes = pl.ds(0, nx), pl.ds(nx, nx)
 
@@ -462,6 +461,8 @@
     def loads(s):
         box, place_in = own_rows(s)
         return [
+            pltpu.make_async_copy(fields, field_box, load_sem.at[4]),
+            pltpu.make_async_copy(code, code_box, load_sem.at[5]),
             pltpu.make_async_copy(bits, bit_box, load_sem.at[0]),
             pltpu.make_async_copy(flag, flag_box, load_sem.at[1]),
             pltpu.make_async_copy(fields.at[:, :, box], raw.at[:, own_planes, place_in], load_sem.at[2]),
@@ -476,8 +477,8 @@
 
     def triple(from_rows, to_planes, to_rows, send, recv, step):
         return [
-            remote(fields.at[:, :, from_rows], raw.at[:, to_planes, to_rows], send.at[0], recv.at[0], step),
-            remote(code.at[:, from_rows], rawcode.at[to_planes, to_rows], send.at[1], recv.at[1], step),
+            remote(field_box.at[:, :, from_rows], raw.at[:, to_planes, to_rows], send.at[0], recv.at[0], step),
+            remote(code_box.at[:, from_rows], rawcode.at[to_planes, to_rows], send.at[1], recv.at[1], step),
             remote(act_box.at[:, from_rows], act.at[0, to_planes, to_rows], send.at[2], recv.at[2], step),
         ]
 
@@ -519,8 +520,13 @@
     def box_rows(s, k):
         return pl.ds(pl.multiple_of(s * half + ROWS * k, ROWS), ROWS)
 
-    def back_copy(k):
-        return remote(done.at[k], out.at[:, :, box_rows(side, k)], back_send.at[k], back_recv.at[k], (1, 0, 0))
+    parts = [(first, size) for first, size in ((0, nx // 2), (nx // 2, nx - nx // 2)) if size]
+
+    def back_copy(k, part):
+        some = pl.ds(*parts[part])
+        return remote(
+            done.at[k, :, some], out.at[:, some, box_rows(side, k)], back_send.at[k, part], back_recv.at[k, part], (1, 0, 0),
+        )
 
     lane = lax.broadcasted_iota(jnp.int32, (ROWS, nz), 1)
     within = jnp.bitwise_and(lane, GROUP - 1)
@@ -537,9 +543,11 @@
         box, place_in = own_rows(s)
         chunks = [x_copies(s, t) for t in order(1 - s)]
         pl.semaphore_wait(barrier, len(near) + not_first.astype(jnp.int32) + not_last.astype(jnp.int32))
+        for copy in copies[:2]:
+            copy.wait()
         for copy in chunks[0][:2]:
             copy.start()
-        for copy in copies[:2]:
+        for copy in copies[2:4]:
             copy.wait()
 
         def plane(x, carry):
@@ -551,6 +559,9 @@
         lax.fori_loop(0, nx, plane, 0, unroll=nx)
         for copy in chunks[0][2:] + sum(chunks[1:], []):
             copy.start()
+
+        for hop in range(counts[1] - 1):
+            pass_tokens(hop)
 
         def keep(x, carry):
             start, end, size = box.start, place_in.start, box.size
@@ -560,11 +571,8 @@
             return carry
 
         lax.fori_loop(0, nx, keep, 0, unroll=nx)
-        for copy in copies[2:]:
+        for copy in copies[4:]:
             copy.wait()
-        meet_rows()
-        for copy in y_copies(s, False) + y_copies(s, True):
-            copy.start()
 
     by_side(begin)
 
@@ -785,8 +793,9 @@
                 out[c, x, rows] = value
             return carry
 
-        lax.fori_loop(0, nx, far, 0, unroll=nx)
-        back_copy(k).start()
+        for part, (start, size) in enumerate(parts):
+            lax.fori_loop(start, start + size, far, 0, unroll=size)
+            back_copy(k, part).start()
         lax.fori_loop(0, nx, near, 0, unroll=nx)
 
     def run(s):
@@ -798,6 +807,17 @@
             def _():
                 arrived(s, tile(u))
                 prepare(tile(u))
+
+            @pl.when(u == 0)
+            def _():
+                pass_tokens(counts[1] - 1)
+                tell(across, (1, 0, 0))
+
+            @pl.when(u == 1)
+            def _():
+                pl.semaphore_wait(across, 1)
+                for copy in y_copies(s, False) + y_copies(s, True):
+                    copy.start()
 
             @pl.when(u > 0)
             def _():
@@ -828,7 +848,8 @@
 
     by_side(drain)
     for k in range(tiles - 1):
-        back_copy(k).wait()
+        for part in range(len(parts)):
+            back_copy(k, part).wait()
 
 
 def folded_body(counts, fields, code, flag, bits):
@@ -853,6 +874,8 @@
         in_specs=[whole] * 4,
         out_specs=pl.BlockSpec(memory_space=pltpu.VMEM),
         scratch_shapes=[
+            pltpu.VMEM((nf, nx, ny, nz), f32),
+            pltpu.VMEM((nx, ny, nz), i32),
             pltpu.VMEM((nf, planes, high, nz), f32),
             pltpu.VMEM((planes, high, nz), i32),
             pltpu.VMEM((nx, ny, nz), i32),
@@ -874,11 +897,11 @@
             pltpu.VMEM((2, nf + 1, depth, nz), f32),
             pltpu.VMEM((2, depth, nz), i32),
             pltpu.VMEM((tiles - 1, nf, nx, ROWS, nz), f32),
-            dma((4,)),
+            dma((6,)),
             dma((tiles, 3)), dma((tiles, 3)),
             dma((2, 3)), dma((2, 3)),
             dma((tiles, 2, 2)), dma((tiles, 2, 2)),
-            dma((tiles - 1,)), dma((tiles - 1,)),
+            dma((tiles - 1, 2)), dma((tiles - 1, 2)),
             pltpu.SemaphoreType.REGULAR((3,)),
         ],
         compiler_params=pltpu.CompilerParams(collective_id=0, has_side_effects=True),

time: 28.9 us -> 27.7 us (0.958)
  Pallas kernels: 28 us -> 26.7 us
    pallas_call x1, Pallas kernels: 28 us -> 26.7 us  [folded_body(): pl.pallas_call(functools.partial(folded_kernel, counts), out_shape=pltpu....]
where the time goes in v4:
time: 27.7 us; the launch traced here: 27.5 us
  Pallas kernels  26.7 us (96%)
  local copies, waits for them, and re-layouts  0.8 us (3%)
    pallas_call x1, Pallas kernels, folded_body(): pl.pallas_call(functools.partial(folded_kernel, counts), out_shape=pltpu....  26.7 us
    unnamed x1, local copies, waits for them, and re-layouts  0.8 us

profile of v4, /device:TPU:0, one launch (start us, length us, event | category | flops | bytes accessed | tf_op | source)
XLA Modules:
  0.0 27.5 jit_solution(12339108798070354435)
XLA Ops:
  0.0 26.7 %shard_map.46 = f32[4,4,64,128]{3,2,1,0:T(8,128)S(1)} custom-call(f32[4,4,64,128]{3,2,1,0:T(8,128)} %fields.1, s32[4,64,128]{2,1,0:T(8,128)} %code.1, s32[4,64,128]{2,1,0:T(8,128)} %flag.1, s32[4,64,128]{2,1,0:T(8,128)} %bits.1), custom_call_target="tpu_custom_call" | custom-call | tf_op jit(solution)/shard_map/pallas_call | solution.py:871
  26.7 0.8 %copy.6 = f32[4,4,64,128]{3,2,1,0:T(8,128)} copy(f32[4,4,64,128]{3,2,1,0:T(8,128)S(1)} %shard_map.46) | data formatting | bytes 1048576

commit v5 on v4

--- a/solution.py
+++ b/solution.py
@@ -399,7 +399,7 @@
 def folded_kernel(
     counts, fields, code, flag, bits, out,
     field_box, code_box, raw, rawcode, bit_box, flag_box, act_box, act, pull0, push0, pull1, push1,
-    edge_act, edge0, edge1, edge2, edge3, ends, act_ends,
+    edge_act, edge0, edge1, edge2, ends, act_ends,
     volume, inverse, weight, edge_volume, edge_weight,
     packed, act_packed, landed, act_landed, done,
     load_sem, x_send, x_recv, y_send, y_recv, z_send, z_recv, back_send, back_recv, token,
@@ -615,10 +615,6 @@
             put(pull0, t, ROWS, 0, x, 0)(kappa)
             for c in range(nf):
                 put(pull0, t, ROWS, 0, x, c + 1)(kappa * get(raw, t, ROWS, c, x))
-            others = ones_in(jnp.bitwise_and(get(act, t, ROWS, 0, x), ((1 << 27) - 1) ^ (1 << 13)))
-            scale = 1.0 / (1 + others).astype(jnp.float32)
-            put(inverse, t, ROWS, x)(scale)
-            put(weight, t, ROWS, x)(scale * kappa)
             return carry
 
         lax.fori_loop(0, planes, plane, 0, unroll=planes)
@@ -635,10 +631,19 @@
         for copy in z_copies(t):
             copy.start()
 
+        def counts_of(x, carry):
+            others = ones_in(jnp.bitwise_and(get(act, t, ROWS, 0, x), ((1 << 27) - 1) ^ (1 << 13)))
+            scale = 1.0 / (1 + others).astype(jnp.float32)
+            put(inverse, t, ROWS, x)(scale)
+            put(weight, t, ROWS, x)(scale * get(pull0, t, ROWS, 0, x, 0))
+            return carry
+
+        lax.fori_loop(0, planes, counts_of, 0, unroll=planes)
+
     turns = [(sx, sz) for sx in (-1, 0, 1) for sz in (-1, 0, 1)]
 
     def spread(tile, keep, keep_end):
-        for v, (sx, sz) in enumerate(turns):
+        for v, (sx, sz) in enumerate(turns if keep else []):
             keep(v)(rolled(tile, -(GROUP * sx + sz)))
         meet = 3 * REACH + 1
         pair = jnp.where(within == meet, rolled(tile, meet - (REACH - 1)), tile)
@@ -740,7 +745,7 @@
             scale = read_volume()
         return [value * scale for value in values]
 
-    sources = ((pull0, edge0), (push0, edge1), (pull1, edge2), (push1, edge3))
+    sources = ((pull0, edge0), (push0, edge1), (pull1, edge2), (push1, None))
 
     def advance(s, stage, t):
         first = ROWS - 1 - stage if s == 1 else ROWS + 1 + stage
@@ -757,7 +762,7 @@
             def keep_end(x, moved):
                 ends[x, c] = moved
 
-            spread(value, lambda v: put(edge_target, t, first, v, c), keep_end)
+            spread(value, None if stage == 2 else lambda v: put(edge_target, t, first, v, c), keep_end)
 
         def plane(x, carry):
             values = plane_values(source, arrays, pulls, t, first, x)
@@ -884,7 +889,7 @@
             pltpu.VMEM((3, planes, high, nz), i32),
             main(nf + 1), main(nf), main(nf), main(nf),
             pltpu.VMEM((9, high, nz), i32),
-            edge(nf + 1), edge(nf), edge(nf), edge(nf),
+            edge(nf + 1), edge(nf), edge(nf),
             pltpu.VMEM((planes, nf + 1, ROWS, nz), f32),
             pltpu.VMEM((planes, ROWS, nz), i32),
             pltpu.VMEM((planes, high, nz), f32),

time: 27.7 us -> 27.6 us (level)
  no operation moved by 1% of the time
where the time goes in v5:
time: 27.6 us; the launch traced here: 27.5 us
  Pallas kernels  26.7 us (97%)
  local copies, waits for them, and re-layouts  0.8 us (3%)
    pallas_call x1, Pallas kernels, folded_body(): pl.pallas_call(functools.partial(folded_kernel, counts), out_shape=pltpu....  26.7 us
    unnamed x1, local copies, waits for them, and re-layouts  0.8 us

profile of v5, /device:TPU:0, one launch (start us, length us, event | category | flops | bytes accessed | tf_op | source)
XLA Modules:
  0.0 27.5 jit_solution(10727871897810028969)
XLA Ops:
  0.0 26.7 %shard_map.46 = f32[4,4,64,128]{3,2,1,0:T(8,128)S(1)} custom-call(f32[4,4,64,128]{3,2,1,0:T(8,128)} %fields.1, s32[4,64,128]{2,1,0:T(8,128)} %code.1, s32[4,64,128]{2,1,0:T(8,128)} %flag.1, s32[4,64,128]{2,1,0:T(8,128)} %bits.1), custom_call_target="tpu_custom_call" | custom-call | tf_op jit(solution)/shard_map/pallas_call | solution.py:876
  26.7 0.8 %copy.6 = f32[4,4,64,128]{3,2,1,0:T(8,128)} copy(f32[4,4,64,128]{3,2,1,0:T(8,128)S(1)} %shard_map.46) | data formatting | bytes 1048576
